TPU v7x, 32 devices: a whole 2x2x4 slice. The times are simulated.
32 devices in a mesh: tile: 8 (over z, x), conv: 4 (over y, core).
Axes of the slice: x: 2, y: 2, z: 4, core: 2. Of those that a mesh axis runs over, the one named last changes fastest.
Arguments:
- field: float32 [256, 24576], P(None, ('tile', 'conv')), may hold values from -6 to 6
- interp: bfloat16 [32768, 384], P(('tile', 'conv')), may hold values from -0.1875 to 0.1875
- conv_blocks: bfloat16 [64, 3, 256, 256], P(('tile', 'conv')), may hold values from -0.21875 to 0.21875
- band_shift: int32 [64, 3], P(('tile', 'conv')), may hold values from 0 to 1
- owner: int32 [12288, 1], P(('tile', 'conv')), may hold values from 0 to 3; in each aligned block of 384 rows (0 to 383, 384 to 767, ...) at most 128 rows name the same one
- edge_index: int32 [64, 128], P(('tile', 'conv')), may hold values from 0 to 767, as said below
Outputs:
- correlated: float32 [256, 24576], P(None, ('tile', 'conv'))
Inputs may be any that keep to these rules, and one draw needn't show every extreme that they name: `edge_index`: row 2b lists the first 128 columns of domain b in some order, row 2b + 1 its last 128 columns in some order. Among the 384 points of one domain no owner is named more than 128 times, and in some domains one owner is named exactly 128 times.
All inputs are finite; a program needn't handle non-finite values.
Results may differ from a plain program's by a relative error of at most 0.0049.
Values may be sent and summed in bfloat16 or wider, within the bound.
A program may use at most 64 MiB of HBM per device.

v0:
```python
import jax
import jax.numpy as jnp
from jax import lax
from jax.sharding import PartitionSpec as P


def padded(cells, sides, width):
    for axis, dim in sides:
        count = lax.axis_size(axis)
        head = lax.slice_in_dim(cells, 0, width, axis=dim)
        tail = lax.slice_in_dim(cells, cells.shape[dim] - width, cells.shape[dim], axis=dim)
        cells = jnp.concatenate(
            [
                lax.ppermute(tail, axis, [(i, (i + 1) % count) for i in range(count)]),
                cells,
                lax.ppermute(head, axis, [((i + 1) % count, i) for i in range(count)]),
            ],
            axis=dim,
        )
    return cells


def contract_last(left_side, right_side):
    return lax.dot_general(
        left_side, right_side, (((1,), (1,)), ((), ())), preferred_element_type=jnp.float32
    )


def convolve(values, conv_blocks, band_shift):
    height = values.shape[0]
    owned_blocks = conv_blocks.shape[0]
    points = conv_blocks.shape[2]
    pieces = values.reshape(height, owned_blocks, points)
    source = (jnp.arange(owned_blocks, dtype=jnp.int32)[:, None] + band_shift) % owned_blocks
    select = (
        source[:, :, None] == jnp.arange(owned_blocks, dtype=jnp.int32)[None, None, :]
    ).astype(jnp.bfloat16)
    picked = jnp.einsum("rsp,jbs->rjbp", pieces, select, preferred_element_type=jnp.float32).astype(
        jnp.bfloat16
    )
    forward = jnp.einsum(
        "rjbp,jbpq->rjq", picked, conv_blocks, preferred_element_type=jnp.float32
    ).astype(jnp.bfloat16)
    backward = jnp.einsum(
        "rjq,jbpq->rjbp", forward, conv_blocks, preferred_element_type=jnp.float32
    )
    adjoint = jnp.einsum(
        "rjbp,jbs->rsp", backward, select.astype(jnp.float32), precision=lax.Precision.HIGHEST
    )
    return adjoint.reshape(height, owned_blocks * points).astype(jnp.bfloat16)


def on_device(field, interp, conv_blocks, band_shift, owner, edge_index):
    columns = field.shape[1]
    rim_width = edge_index.shape[1]
    groups = lax.axis_size("conv")
    slot_count = conv_blocks.shape[0] * conv_blocks.shape[2]
    capacity = slot_count // groups
    rounded = field.astype(jnp.bfloat16)
    left_list = edge_index[0]
    right_list = edge_index[1]
    rim_values = jnp.concatenate(
        [jnp.take(rounded, left_list, axis=1), jnp.take(rounded, right_list, axis=1)], axis=1
    )
    widened = padded(rim_values, ((("tile", "conv"), 1),), rim_width)
    from_left = widened[:, :rim_width]
    from_right = widened[:, 3 * rim_width :]
    extended = jnp.concatenate([from_left, rounded, from_right], axis=1)
    subgrid = jnp.dot(extended, interp, preferred_element_type=jnp.float32)
    subgrid = subgrid.astype(jnp.bfloat16)
    owners = owner[:, 0]
    choose = (owners[:, None] == jnp.arange(groups, dtype=jnp.int32)[None, :]).astype(jnp.int32)
    before = jnp.cumsum(choose, axis=0) - choose
    position = jnp.sum(before * choose, axis=1)
    slot_index = owners * capacity + position
    placement = (slot_index[:, None] == jnp.arange(slot_count, dtype=jnp.int32)[None, :]).astype(
        jnp.bfloat16
    )
    outgoing = jnp.dot(subgrid, placement, preferred_element_type=jnp.float32).astype(jnp.bfloat16)
    incoming = lax.all_to_all(
        convolve(
            lax.all_to_all(outgoing, "conv", split_axis=1, concat_axis=1, tiled=True),
            conv_blocks,
            band_shift,
        ),
        "conv",
        split_axis=1,
        concat_axis=1,
        tiled=True,
    )
    returned = contract_last(incoming, placement).astype(jnp.bfloat16)
    partial_value = contract_last(returned, interp)
    left_part = partial_value[:, :rim_width]
    right_part = partial_value[:, rim_width + columns :]
    edge_sums = padded(
        jnp.concatenate([left_part, right_part], axis=1).astype(jnp.bfloat16),
        ((("tile", "conv"), 1),),
        rim_width,
    ).astype(jnp.float32)
    interior_part = partial_value[:, rim_width : rim_width + columns]
    result = interior_part.at[:, left_list].add(edge_sums[:, :rim_width])
    result = result.at[:, right_list].add(edge_sums[:, 3 * rim_width :])
    return result


def solution(mesh):
    return jax.shard_map(
        on_device,
        mesh=mesh,
        in_specs=(
            P(None, ("tile", "conv")),
            P(("tile", "conv"), None),
            P(("tile", "conv"), None, None, None),
            P(("tile", "conv"), None),
            P(("tile", "conv"), None),
            P(("tile", "conv"), None),
        ),
        out_specs=P(None, ("tile", "conv")),
        check_vma=False,
    )
```

profile of v0, /device:TPU:0, one launch (start us, length us, event | category | flops | bytes accessed | tf_op | source)
XLA Modules:
  0.0 51.1 jit_solution(18035988229664410516)
XLA Ops:
  0.0 0.0 copy-start
  0.0 0.0 copy-start.1
  0.0 0.8 %compare_and_fusion.1 = (pred[128]{0:T(512)(128)(4,1)S(1)}, s32[128]{0:T(128)S(1)}, pred[128]{0:T(512)(128)(4,1)S(1)}, s32[128]{0:T(128)S(1)}) fusion(s32[2,128]{1,0:T(2,128)} %param.13), kind=kLoop, calls=%fused_computation.58 | loop fusion | flops 1536 | bytes 2304 | tf_op jit(solution)/shard_map/jit(_take)/and | solution.py:63
  0.8 1.3 %copy.27 = bf16[256,768]{0,1:T(8,128)(2,1)S(1)} copy(f32[256,768]{1,0:T(8,128)} %param.8) | data formatting | bytes 1179648 | tf_op args[0]
  2.1 0.8 %gather_fusion = bf16[128,256]{1,0:T(8,128)(2,1)S(1)} fusion(bf16[256,768]{0,1:T(8,128)(2,1)S(1)} %copy.27, s32[1024]{0:T(1024)S(1)} %pad_clamp_fusion.1), kind=kCustom, calls=%fused_computation.clone | custom fusion | bytes 131584 | tf_op jit(solution)/shard_map/jit(_take)/gather | solution.py:63
  3.0 0.1 select_bitcast_fusion.1
  3.1 0.5 %collective-permute-start = (bf16[256,128]{0,1:T(8,128)(2,1)S(1)}, bf16[256,128]{0,1:T(8,128)(2,1)S(1)}, u32[]{:S(2)}, u32[]{:S(2)}) collective-permute-start(bf16[256,128]{0,1:T(8,128)(2,1)S(1)} %select_bitcast_fusion.1), channel_id=1, source_target_pairs={{0,1},{1,2},{2,3},{3,4},{4,5},{5,6},{6,7},{7,8},{8,9},{9,10},{10,1... | collective-permute-start | bytes 196616 | tf_op jit(solution)/shard_map/ppermute | solution.py:14
  3.6 0.8 %gather_fusion.1 = bf16[128,256]{1,0:T(8,128)(2,1)S(1)} fusion(bf16[256,768]{0,1:T(8,128)(2,1)S(1)} %copy.27, s32[1024]{0:T(1024)S(1)} %pad_clamp_fusion), kind=kCustom, calls=%fused_computation.1.clone | custom fusion | bytes 131584 | tf_op jit(solution)/shard_map/jit(_take)/gather | solution.py:63
  4.5 0.1 select_bitcast_fusion
  4.5 6.0 %collective-permute-start.1 = (bf16[256,128]{0,1:T(8,128)(2,1)S(1)}, bf16[256,128]{0,1:T(8,128)(2,1)S(1)}, u32[]{:S(2)}, u32[]{:S(2)}) collective-permute-start(bf16[256,128]{0,1:T(8,128)(2,1)S(1)} %select_bitcast_fusion), channel_id=1, source_target_pairs={{1,0},{2,1},{3,2},{4,3},{5,4},{6,5},{7,6},{8,7},{9,8},{10,9},{11,1... | collective-permute-start | bytes 196616 | tf_op jit(solution)/shard_map/ppermute | solution.py:16
  10.5 0.0 copy-done.1
  10.6 1.2 %reduce-window.6 = s32[4,3,128]{2,1,0:T(4,128)S(1)} reduce-window(s32[4,3,128]{2,1,0:T(4,128)S(1)} %fusion.32, s32[]{:T(128)} %constant.30.clone.1), window={size=1x1x128 pad=0_0x0_0x127_0}, to_apply=%region_0.0 | reduce-window | flops 195072 | bytes 12292 | tf_op jit(solution)/shard_map/reduce-window
  11.8 0.2 slice_reduce_fusion
  12.0 0.2 reduce-window.9
  12.2 0.1 add_bitcast_fusion
  12.3 0.0 copy-start.3
  12.3 0.0 collective-permute-done
  12.3 0.1 collective-permute-done.1
  12.4 0.0 copy-done
  12.4 0.7 %fusion.10 = bf16[32,4,8,128]{3,2,1,0:T(8,128)(2,1)S(1)} fusion(bf16[1024,384]{1,0:T(8,128)(2,1)S(1)} %copy-done, bf16[256,128]{0,1:T(8,128)(2,1)S(1)} %collective-permute-done.1, bf16[256,768]{0,1:T(8,128)(2,1)S(1)} %copy.27, bf16[256,128]{0,1:T(8,128)(2,1)S(1)} %collective-permute-done, s32[384]{0:T(512)S(1)} %add_reduce_fusion), kind=kOutput, calls=%fused_computation.16 | convolution fusion | flops 303988736 | bytes 1574400 | tf_op jit(solution)/shard_map/dot_general | solution.py:79
  13.1 0.7 %copy.58 = bf16[32,4,8,128]{3,2,0,1:T(8,128)(2,1)} copy(bf16[32,4,8,128]{3,2,1,0:T(8,128)(2,1)S(1)} %fusion.10) | data formatting | bytes 524288 | tf_op jit(solution)/shard_map/all_to_all | solution.py:82
  13.9 3.4 %all-to-all-start = ((bf16[256,4,128]{2,0,1:T(8,128)(2,1)}), bf16[256,4,128]{2,0,1:T(8,128)(2,1)S(1)}, u32[]{:S(2)}, u32[]{:S(2)}) async-start(bf16[256,4,128]{2,0,1:T(8,128)(2,1)} %bitcast.89), calls=%async_computation | async-start | bytes 524288 | tf_op jit(solution)/shard_map/all_to_all | solution.py:82
  17.3 0.0 copy-done.3
  17.3 5.9 %all-to-all-done = bf16[256,4,128]{2,0,1:T(8,128)(2,1)S(1)} async-done(((bf16[256,4,128]{2,0,1:T(8,128)(2,1)}), bf16[256,4,128]{2,0,1:T(8,128)(2,1)S(1)}, u32[]{:S(2)}, u32[]{:S(2)}) %all-to-all-start) | async-done | bytes 262176 | tf_op jit(solution)/shard_map/all_to_all | solution.py:82
  23.3 0.2 copy.29
  23.5 0.2 reshape.131
  23.7 1.0 %fusion.2 = bf16[256,2,3,256]{3,2,0,1:T(4,128)(2,1)S(1)} fusion(bf16[256,2,256,1]{2,1,0,3:T(2,128)(2,1)S(1)} %reshape.131, s32[2,3]{1,0:T(2,128)S(1)} %and_select_fusion), kind=kOutput, calls=%fused_computation.8 | convolution fusion | flops 1966092 | bytes 1048600 | tf_op jit(solution)/shard_map/rsp,jbs->rjbp/dot_general | solution.py:38
  24.7 2.0 %convolution_bitcast_fusion = f32[256,2,3,256]{3,0,2,1:T(8,128)S(1)} fusion(bf16[2,3,256,256]{3,2,1,0:T(8,128)(2,1)} %param.10, bf16[256,2,3,256]{3,2,0,1:T(4,128)(2,1)S(1)} %fusion.2), kind=kOutput, calls=%fused_computation.6 | convolution fusion | flops 402784256 | bytes 3145728 | tf_op jit(solution)/shard_map/rjq,jbpq->rjbp/dot_general | solution.py:44
  26.7 2.9 %fusion.11 = bf16[256,2,256]{2,1,0:T(2,128)(2,1)S(1)} fusion(f32[256,2,3,256]{3,0,2,1:T(8,128)S(1)} %convolution_bitcast_fusion, s32[2,3]{1,0:T(2,128)S(1)} %and_select_fusion), kind=kOutput, calls=%fused_computation.17 | convolution fusion | flops 9568268 | bytes 1835032 | tf_op jit(solution)/shard_map/rjbp,jbs->rsp/dot_general | solution.py:47
  29.6 0.2 convert_element_type.59
  29.9 8.4 %all_to_all.18 = bf16[256,4,128]{2,0,1:T(8,128)(2,1)S(1)} all-to-all(bf16[256,4,128]{2,0,1:T(8,128)(2,1)S(1)} %copy.32), channel_id=1, replica_groups=mesh['tile'=8,'conv'=4] {'conv'}, dimensions={1} | all-to-all | bytes 524288 | tf_op jit(solution)/shard_map/all_to_all | solution.py:80
  38.3 0.1 copy.33
  38.4 0.0 copy-start.2
  38.4 0.8 %fusion.46 = (bf16[256,1024]{1,0:T(8,128)(2,1)S(1)}, f32[256,1024]{1,0:T(8,128)S(1)}) fusion(bf16[1024,384]{1,0:T(8,128)(2,1)S(1)} %copy-done, bf16[256,512]{0,1:T(8,128)(2,1)S(1)} %bitcast.91, s32[384]{0:T(512)S(1)} %add_reduce_fusion), kind=kOutput, calls=%fused_computation.68 | convolution fusion | flops 302546944 | bytes 2622976 | tf_op jit(solution)/shard_map/dot_general | solution.py:24
  39.2 0.1 collective-permute-start.2
  39.3 5.3 %collective-permute-start.3 = (bf16[256,128]{1,0:T(8,128)(2,1)S(1)}, bf16[256,128]{1,0:T(8,128)(2,1)S(1)}, u32[]{:S(2)}, u32[]{:S(2)}) collective-permute-start(bf16[256,128]{1,0:T(8,128)(2,1)S(1)} %get-tuple-element.11), channel_id=1, source_target_pairs={{1,0},{2,1},{3,2},{4,3},{5,4},{6,5},{7,6},{8,7},{9,8},{10,9},{11,1... | collective-permute-start | bytes 196616 | tf_op jit(solution)/shard_map/ppermute | solution.py:16
  44.6 0.0 copy-done.2
  44.6 0.1 slice.45
  44.7 0.3 copy.34
  45.0 1.6 %collective-permute-done.2 = bf16[256,128]{1,0:T(8,128)(2,1)S(1)} collective-permute-done((bf16[256,128]{1,0:T(8,128)(2,1)S(1)}, bf16[256,128]{1,0:T(8,128)(2,1)S(1)}, u32[]{:S(2)}, u32[]{:S(2)}) %collective-permute-start.2) | collective-permute-done | bytes 65568 | tf_op jit(solution)/shard_map/ppermute | solution.py:14
  46.6 0.0 collective-permute-done.3
  46.6 0.1 copy.35
  46.7 0.1 copy.36
  46.8 1.6 %scatter_fusion = f32[256,768]{0,1:T(8,128)S(1)} fusion(f32[256,768]{0,1:T(8,128)S(1)} %copy.34, s32[128]{0:T(128)S(1)} %get-tuple-element.15, f32[128,256]{1,0:T(8,128)S(1)} %copy.35), kind=kCustom, calls=%fused_computation.2 | custom fusion | flops 32768 | bytes 393728 | tf_op jit(solution)/shard_map/scatter-add | solution.py:101
  48.4 1.6 %scatter_fusion.1 = f32[256,768]{0,1:T(8,128)S(1)} fusion(f32[256,768]{0,1:T(8,128)S(1)} %scatter_fusion, s32[128]{0:T(128)S(1)} %get-tuple-element.14, f32[128,256]{1,0:T(8,128)S(1)} %copy.36), kind=kCustom, calls=%fused_computation.3 | custom fusion | flops 32768 | bytes 393728 | tf_op jit(solution)/shard_map/scatter-add | solution.py:102
  50.0 1.1 %copy.37 = f32[256,768]{1,0:T(8,128)} copy(f32[256,768]{0,1:T(8,128)S(1)} %scatter_fusion.1) | data formatting | bytes 1572864 | tf_op jit(solution)/shard_map/scatter-add | solution.py:102
  (11 shorter events, 0.2 us)
Async XLA Ops:
  0.0 12.4 %copy-start = (bf16[1024,384]{1,0:T(8,128)(2,1)S(1)}, bf16[1024,384]{1,0:T(8,128)(2,1)}, u32[]{:S(2)}) copy-start(bf16[1024,384]{1,0:T(8,128)(2,1)} %param.9) | copy-start | bytes 2359300
  0.0 10.5 %copy-start.1 = (s32[384,1]{0,1:T(1,128)S(1)}, s32[384,1]{0,1:T(1,128)}, u32[]{:S(2)}) copy-start(s32[384,1]{0,1:T(1,128)} %param.12) | copy-start | bytes 4612
  3.1 9.3 %collective-permute-start = (bf16[256,128]{0,1:T(8,128)(2,1)S(1)}, bf16[256,128]{0,1:T(8,128)(2,1)S(1)}, u32[]{:S(2)}, u32[]{:S(2)}) collective-permute-start(bf16[256,128]{0,1:T(8,128)(2,1)S(1)} %select_bitcast_fusion.1), channel_id=1, source_target_pairs={{0,1},{1,2},{2,3},{3,4},{4,5},{5,6},{6,7},{7,8},{8,9},{9,10},{10,1... | collective-permute-start | bytes 196616 | tf_op jit(solution)/shard_map/ppermute | solution.py:14
  4.5 7.9 %collective-permute-start.1 = (bf16[256,128]{0,1:T(8,128)(2,1)S(1)}, bf16[256,128]{0,1:T(8,128)(2,1)S(1)}, u32[]{:S(2)}, u32[]{:S(2)}) collective-permute-start(bf16[256,128]{0,1:T(8,128)(2,1)S(1)} %select_bitcast_fusion), channel_id=1, source_target_pairs={{1,0},{2,1},{3,2},{4,3},{5,4},{6,5},{7,6},{8,7},{9,8},{10,9},{11,1... | collective-permute-start | bytes 196616 | tf_op jit(solution)/shard_map/ppermute | solution.py:16
  12.3 5.0 %copy-start.3 = (s32[2,3]{1,0:T(2,128)S(1)}, s32[2,3]{1,0:T(2,128)}, u32[]{:S(2)}) copy-start(s32[2,3]{1,0:T(2,128)} %param.11) | copy-start | bytes 76
  13.9 9.4 %all-to-all-start = ((bf16[256,4,128]{2,0,1:T(8,128)(2,1)}), bf16[256,4,128]{2,0,1:T(8,128)(2,1)S(1)}, u32[]{:S(2)}, u32[]{:S(2)}) async-start(bf16[256,4,128]{2,0,1:T(8,128)(2,1)} %bitcast.89), calls=%async_computation | async-start | bytes 524288 | tf_op jit(solution)/shard_map/all_to_all | solution.py:82
  38.4 6.2 %copy-start.2 = (s32[2,128]{1,0:T(2,128)S(1)}, s32[2,128]{1,0:T(2,128)}, u32[]{:S(2)}) copy-start(s32[2,128]{1,0:T(2,128)} %param.13) | copy-start | bytes 3076
  39.2 7.3 %collective-permute-start.2 = (bf16[256,128]{1,0:T(8,128)(2,1)S(1)}, bf16[256,128]{1,0:T(8,128)(2,1)S(1)}, u32[]{:S(2)}, u32[]{:S(2)}) collective-permute-start(bf16[256,128]{1,0:T(8,128)(2,1)S(1)} %get-tuple-element.10), channel_id=1, source_target_pairs={{0,1},{1,2},{2,3},{3,4},{4,5},{5,6},{6,7},{7,8},{8,9},{9,10},{10,1... | collective-permute-start | bytes 196616 | tf_op jit(solution)/shard_map/ppermute | solution.py:14
  39.3 7.3 %collective-permute-start.3 = (bf16[256,128]{1,0:T(8,128)(2,1)S(1)}, bf16[256,128]{1,0:T(8,128)(2,1)S(1)}, u32[]{:S(2)}, u32[]{:S(2)}) collective-permute-start(bf16[256,128]{1,0:T(8,128)(2,1)S(1)} %get-tuple-element.11), channel_id=1, source_target_pairs={{1,0},{2,1},{3,2},{4,3},{5,4},{6,5},{7,6},{8,7},{9,8},{10,9},{11,1... | collective-permute-start | bytes 196616 | tf_op jit(solution)/shard_map/ppermute | solution.py:16
where the time goes:
time: 51.4 us; the launch traced here: 51.1 us
  starting transfers between devices  15.3 us (30%)
  blocking collectives  8.39 us (16%)
  waiting for transfers between devices  7.66 us (15%)
  matrix products  7.43 us (14%)
  local copies, waits for them, and re-layouts  6.38 us (12%)
  other arithmetic  5.73 us (11%)
    ppermute x2, starting transfers between devices, padded(): lax.ppermute(head, axis, [((i + 1) % count, i) for i in range(count)])  11.3 us
    all_to_all x1, blocking collectives, on_device(): lax.all_to_all(convolve(lax.all_to_all(outgoing, 'conv', split_axis=1, co...  8.39 us
    all_to_all x1, waiting for transfers between devices, on_device(): lax.all_to_all(outgoing, 'conv', split_axis=1, concat_axis=1, tiled=True)  5.95 us
    all_to_all x1, starting transfers between devices, on_device(): lax.all_to_all(outgoing, 'conv', split_axis=1, concat_axis=1, tiled=True)  3.41 us
    dot_general x1, matrix products, convolve(): jnp.einsum('rjbp,jbs->rsp', backward, select.astype(jnp.float32), precisi...  2.94 us
    dot_general x1, matrix products, convolve(): jnp.einsum('rjq,jbpq->rjbp', forward, conv_blocks, preferred_element_type...  2.02 us
    ppermute x2, waiting for transfers between devices, padded(): lax.ppermute(tail, axis, [(i, (i + 1) % count) for i in range(count)])  1.61 us
    scatter-add x1, other arithmetic, on_device(): result = interior_part.at[:, left_list].add(edge_sums[:, :rim_width])  1.59 us
  transfers between devices with their start and end apart: 5, of which 3 were waited for; matrix products, arithmetic and copies ran while one was open for 6% of the time, Pallas kernels for 0%

commit v1 on v0

--- a/solution.py
+++ b/solution.py
@@ -2,6 +2,29 @@
 import jax.numpy as jnp
 from jax import lax
 from jax.sharding import PartitionSpec as P
+
+
+def in_blocks(x, dim, devices):
+    dims = x.shape
+    tiles = x.reshape(*dims[:dim], devices, dims[dim] // devices, *dims[dim + 1 :])
+    return jnp.moveaxis(tiles, dim, 0)
+
+
+def in_order(blocks, dim):
+    shape = list(blocks.shape[1:])
+    shape[dim] *= blocks.shape[0]
+    return jnp.moveaxis(blocks, 0, dim).reshape(shape)
+
+
+def sent_to_each(x, axis, split_dim, concat_dim):
+    size, index = (lax.axis_size(axis), lax.axis_index(axis))
+    blocks = in_blocks(x, split_dim, size)
+    outs = [blocks[index]]
+    for turn in range(1, size):
+        sent = blocks[(index + turn) % size]
+        outs.append(lax.ppermute(sent, axis, [(i, (i + turn) % size) for i in range(size)]))
+    blocks = jnp.stack(outs)[(index - jnp.arange(size)) % size]
+    return in_order(blocks, concat_dim)
 
 
 def padded(cells, sides, width):
@@ -78,11 +101,7 @@
     )
     outgoing = jnp.dot(subgrid, placement, preferred_element_type=jnp.float32).astype(jnp.bfloat16)
     incoming = lax.all_to_all(
-        convolve(
-            lax.all_to_all(outgoing, "conv", split_axis=1, concat_axis=1, tiled=True),
-            conv_blocks,
-            band_shift,
-        ),
+        convolve(sent_to_each(outgoing, "conv", 1, 1), conv_blocks, band_shift),
         "conv",
         split_axis=1,
         concat_axis=1,

time: 51.4 us -> 47.6 us (0.926)
  starting transfers between devices: 15.3 us -> 12.6 us
  waiting for transfers between devices: 7.66 us -> 6.01 us
    all_to_all x1 -> x0, waiting for transfers between devices: 5.95 us -> none  [on_device(): lax.all_to_all(outgoing, 'conv', split_axis=1, concat_axis=1, tiled=True)]
    ppermute x0 -> x3, waiting for transfers between devices: none -> 4.34 us  [sent_to_each(): lax.ppermute(sent, axis, [(i, (i + turn) % size) for i in range(size)])]
    all_to_all x1 -> x0, starting transfers between devices: 3.41 us -> none  [on_device(): lax.all_to_all(outgoing, 'conv', split_axis=1, concat_axis=1, tiled=True)]
    all_to_all x3 -> x1, local copies, waits for them, and re-layouts: 1.1 us -> 0.14 us  [on_device(): lax.all_to_all(convolve(sent_to_each(outgoing, 'conv', 1, 1), conv_blocks...]
    another operation x0 -> x2, local copies, waits for them, and re-layouts: none -> 0.73 us
    ppermute x0 -> x3, starting transfers between devices: none -> 0.7 us  [sent_to_each(): lax.ppermute(sent, axis, [(i, (i + turn) % size) for i in range(size)])]
    gather x0 -> x1, local copies, waits for them, and re-layouts: none -> 0.6 us  [sent_to_each(): blocks = jnp.stack(outs)[(index - jnp.arange(size)) % size]]
    unnamed x9 -> x13, local copies, waits for them, and re-layouts: 1.32 us -> 1.37 us
  transfers between devices with their start and end apart: 5 -> 7, of which waited for: 3 -> 4; matrix products, arithmetic and copies ran while one was open for 6% -> 7% of each run, Pallas kernels for 0% -> 0%
where the time goes in v1:
time: 47.6 us; the launch traced here: 47.4 us
  starting transfers between devices  12.6 us (26%)
  blocking collectives  8.39 us (18%)
  matrix products  7.44 us (16%)
  local copies, waits for them, and re-layouts  6.84 us (14%)
  waiting for transfers between devices  6.01 us (13%)
  other arithmetic  5.77 us (12%)
    ppermute x2, starting transfers between devices, padded(): lax.ppermute(head, axis, [((i + 1) % count, i) for i in range(count)])  11.3 us
    all_to_all x1, blocking collectives, on_device(): lax.all_to_all(convolve(sent_to_each(outgoing, 'conv', 1, 1), conv_blocks...  8.39 us
    ppermute x3, waiting for transfers between devices, sent_to_each(): lax.ppermute(sent, axis, [(i, (i + turn) % size) for i in range(size)])  4.34 us
    dot_general x1, matrix products, convolve(): jnp.einsum('rjbp,jbs->rsp', backward, select.astype(jnp.float32), precisi...  2.94 us
    dot_general x1, matrix products, convolve(): jnp.einsum('rjq,jbpq->rjbp', forward, conv_blocks, preferred_element_type...  2.02 us
    ppermute x2, waiting for transfers between devices, padded(): lax.ppermute(tail, axis, [(i, (i + 1) % count) for i in range(count)])  1.61 us
    scatter-add x1, other arithmetic, on_device(): result = interior_part.at[:, left_list].add(edge_sums[:, :rim_width])  1.59 us
    scatter-add x1, other arithmetic, on_device(): result = result.at[:, right_list].add(edge_sums[:, 3 * rim_width:])  1.59 us
  transfers between devices with their start and end apart: 7, of which 4 were waited for; matrix products, arithmetic and copies ran while one was open for 7% of the time, Pallas kernels for 0%

profile of v1, /device:TPU:0, one launch (start us, length us, event | category | flops | bytes accessed | tf_op | source)
XLA Modules:
  0.0 47.4 jit_solution(10253065926290474254)
XLA Ops:
  0.0 0.0 copy-start
  0.0 0.8 %compare_and_fusion.1 = (pred[128]{0:T(512)(128)(4,1)S(1)}, s32[128]{0:T(128)S(1)}, pred[128]{0:T(512)(128)(4,1)S(1)}, s32[128]{0:T(128)S(1)}) fusion(s32[2,128]{1,0:T(2,128)} %param.13), kind=kLoop, calls=%fused_computation.67 | loop fusion | flops 1536 | bytes 2304 | tf_op jit(solution)/shard_map/jit(_take)/and | solution.py:86
  0.8 1.3 %copy.36 = bf16[256,768]{0,1:T(8,128)(2,1)S(1)} copy(f32[256,768]{1,0:T(8,128)} %param.8) | data formatting | bytes 1179648 | tf_op args[0]
  2.1 0.8 %gather_fusion.1 = bf16[128,256]{1,0:T(8,128)(2,1)S(1)} fusion(bf16[256,768]{0,1:T(8,128)(2,1)S(1)} %copy.36, s32[1024]{0:T(1024)S(1)} %pad_clamp_fusion.2), kind=kCustom, calls=%fused_computation.clone | custom fusion | bytes 131584 | tf_op jit(solution)/shard_map/jit(_take)/gather | solution.py:86
  2.9 0.1 select_bitcast_fusion.1
  3.0 0.6 %collective-permute-start = (bf16[256,128]{0,1:T(8,128)(2,1)S(1)}, bf16[256,128]{0,1:T(8,128)(2,1)S(1)}, u32[]{:S(2)}, u32[]{:S(2)}) collective-permute-start(bf16[256,128]{0,1:T(8,128)(2,1)S(1)} %select_bitcast_fusion.1), channel_id=1, source_target_pairs={{0,1},{1,2},{2,3},{3,4},{4,5},{5,6},{6,7},{7,8},{8,9},{9,10},{10,1... | collective-permute-start | bytes 196616 | tf_op jit(solution)/shard_map/ppermute | solution.py:37
  3.6 0.8 %gather_fusion.2 = bf16[128,256]{1,0:T(8,128)(2,1)S(1)} fusion(bf16[256,768]{0,1:T(8,128)(2,1)S(1)} %copy.36, s32[1024]{0:T(1024)S(1)} %pad_clamp_fusion.1), kind=kCustom, calls=%fused_computation.1.clone | custom fusion | bytes 131584 | tf_op jit(solution)/shard_map/jit(_take)/gather | solution.py:86
  4.4 0.1 select_bitcast_fusion
  4.5 6.0 %collective-permute-start.1 = (bf16[256,128]{0,1:T(8,128)(2,1)S(1)}, bf16[256,128]{0,1:T(8,128)(2,1)S(1)}, u32[]{:S(2)}, u32[]{:S(2)}) collective-permute-start(bf16[256,128]{0,1:T(8,128)(2,1)S(1)} %select_bitcast_fusion), channel_id=1, source_target_pairs={{1,0},{2,1},{3,2},{4,3},{5,4},{6,5},{7,6},{8,7},{9,8},{10,9},{11,1... | collective-permute-start | bytes 196616 | tf_op jit(solution)/shard_map/ppermute | solution.py:39
  10.5 0.0 copy-done.1
  10.6 1.2 %reduce-window.6 = s32[4,3,128]{2,1,0:T(4,128)S(1)} reduce-window(s32[4,3,128]{2,1,0:T(4,128)S(1)} %fusion.32, s32[]{:T(128)} %constant.63.clone.1), window={size=1x1x128 pad=0_0x0_0x127_0}, to_apply=%region_0.0 | reduce-window | flops 195072 | bytes 12292 | tf_op jit(solution)/shard_map/reduce-window
  11.8 0.2 slice_reduce_fusion
  12.0 0.2 reduce-window.9
  12.2 0.1 add_bitcast_fusion
  12.3 0.0 copy-done.3
  12.4 0.0 collective-permute-done
  12.4 0.1 collective-permute-done.1
  12.4 0.7 %convolution_convert_fusion.1 = bf16[256,512]{1,0:T(8,128)(2,1)S(1)} fusion(bf16[1024,384]{1,0:T(8,128)(2,1)S(1)} %copy-done, bf16[256,128]{0,1:T(8,128)(2,1)S(1)} %collective-permute-done.1, bf16[256,768]{0,1:T(8,128)(2,1)S(1)} %copy.36, bf16[256,128]{0,1:T(8,128)(2,1)S(1)} %collective-permute-done, s32[384]{0:T(512)S(1)} %add_reduce_fusion), kind=kOutput, calls=%fused_computation.12 | convolution fusion | flops 303988736 | bytes 1574400 | tf_op jit(solution)/shard_map/dot_general | solution.py:102
  13.1 0.1 reshape.144
  13.2 0.6 %constant_dynamic-slice_fusion.3 = (bf16[256,1,128]{2,1,0:T(2,128)(2,1)S(1)}, bf16[256,1,128]{2,1,0:T(2,128)(2,1)S(1)}, bf16[256,1,128]{2,1,0:T(2,128)(2,1)S(1)}, bf16[256,1,128]{2,1,0:T(2,128)(2,1)S(1)}) fusion(bf16[256,4,128]{2,1,0:T(4,128)(2,1)S(1)} %reshape.144, s32[]{:T(128)S(6)} %select_n.84, s32[]{:T(128)S(6)} %select_n.88, s32[]{:T(128)S(6)} %select_n.86, ...), kind=kLoop, calls=%fused_computation.77 | loop fusion | bytes 524304 | tf_op jit(solution)/shard_map/dynamic-slice
  13.8 0.1 collective-permute-start.3
  13.9 0.6 %collective-permute-start.4 = (bf16[256,128]{1,0:T(8,128)(2,1)S(1)}, bf16[256,128]{1,0:T(8,128)(2,1)S(1)}, u32[]{:S(2)}, u32[]{:S(2)}) collective-permute-start(bf16[256,128]{1,0:T(8,128)(2,1)S(1)} %bitcast.112), channel_id=1, source_target_pairs={{0,3},{1,0},{2,1},{3,2},{4,7},{5,4},{6,5},{7,6},{8,11},{9,8},{10,9... | collective-permute-start | bytes 196616 | tf_op jit(solution)/shard_map/ppermute | solution.py:25
  14.5 0.1 collective-permute-start.2
  14.6 4.2 %collective-permute-done.3 = bf16[256,128]{1,0:T(8,128)(2,1)S(1)} collective-permute-done((bf16[256,128]{1,0:T(8,128)(2,1)S(1)}, bf16[256,128]{1,0:T(8,128)(2,1)S(1)}, u32[]{:S(2)}, u32[]{:S(2)}) %collective-permute-start.3) | collective-permute-done | bytes 65568 | tf_op jit(solution)/shard_map/ppermute | solution.py:25
  18.7 0.0 collective-permute-done.4
  18.7 0.2 collective-permute-done.2
  18.9 0.6 %gather_fusion = bf16[4,256,128]{2,1,0:T(8,128)(2,1)S(1)} fusion(bf16[4,256,128]{2,1,0:T(8,128)(2,1)S(1)} %pad_maximum_fusion, s32[1024]{0:T(1024)S(1)} %pad_clamp_fusion), kind=kCustom, calls=%fused_computation.2 | custom fusion | bytes 524304 | tf_op jit(solution)/shard_map/gather | solution.py:26
  19.5 0.1 copy.41
  19.7 0.2 copy.42
  19.9 1.0 %fusion.2 = bf16[256,2,3,256]{3,2,0,1:T(4,128)(2,1)S(1)} fusion(bf16[256,2,256]{2,1,0:T(2,128)(2,1)S(1)} %copy.42, s32[2,3]{1,0:T(2,128)S(1)} %and_select_fusion.1), kind=kOutput, calls=%fused_computation.9 | convolution fusion | flops 1966092 | bytes 1048600 | tf_op jit(solution)/shard_map/rsp,jbs->rjbp/dot_general | solution.py:61
  20.9 2.0 %convolution_bitcast_fusion = f32[256,2,3,256]{3,0,2,1:T(8,128)S(1)} fusion(bf16[2,3,256,256]{3,2,1,0:T(8,128)(2,1)} %param.10, bf16[256,2,3,256]{3,2,0,1:T(4,128)(2,1)S(1)} %fusion.2), kind=kOutput, calls=%fused_computation.7 | convolution fusion | flops 402784256 | bytes 3145728 | tf_op jit(solution)/shard_map/rjq,jbpq->rjbp/dot_general | solution.py:67
  22.9 2.9 %fusion.10 = bf16[256,2,256]{2,1,0:T(2,128)(2,1)S(1)} fusion(f32[256,2,3,256]{3,0,2,1:T(8,128)S(1)} %convolution_bitcast_fusion, s32[2,3]{1,0:T(2,128)S(1)} %and_select_fusion.1), kind=kOutput, calls=%fused_computation.17 | convolution fusion | flops 9568268 | bytes 1835032 | tf_op jit(solution)/shard_map/rjbp,jbs->rsp/dot_general | solution.py:70
  25.9 0.2 convert_element_type.59
  26.1 8.4 %all_to_all.9 = bf16[256,4,128]{2,0,1:T(8,128)(2,1)S(1)} all-to-all(bf16[256,4,128]{2,0,1:T(8,128)(2,1)S(1)} %copy.45), channel_id=1, replica_groups=mesh['tile'=8,'conv'=4] {'conv'}, dimensions={1} | all-to-all | bytes 524288 | tf_op jit(solution)/shard_map/all_to_all | solution.py:103
  34.5 0.1 copy.46
  34.6 0.0 copy-start.2
  34.6 0.8 %fusion.48 = (bf16[256,1024]{1,0:T(8,128)(2,1)S(1)}, f32[256,1024]{1,0:T(8,128)S(1)}) fusion(bf16[1024,384]{1,0:T(8,128)(2,1)S(1)} %copy-done, bf16[256,512]{0,1:T(8,128)(2,1)S(1)} %bitcast.107, s32[384]{0:T(512)S(1)} %add_reduce_fusion), kind=kOutput, calls=%fused_computation.84 | convolution fusion | flops 302546944 | bytes 2622976 | tf_op jit(solution)/shard_map/dot_general | solution.py:47
  35.5 0.1 collective-permute-start.5
  35.5 5.3 %collective-permute-start.6 = (bf16[256,128]{1,0:T(8,128)(2,1)S(1)}, bf16[256,128]{1,0:T(8,128)(2,1)S(1)}, u32[]{:S(2)}, u32[]{:S(2)}) collective-permute-start(bf16[256,128]{1,0:T(8,128)(2,1)S(1)} %get-tuple-element.11), channel_id=1, source_target_pairs={{1,0},{2,1},{3,2},{4,3},{5,4},{6,5},{7,6},{8,7},{9,8},{10,9},{11,1... | collective-permute-start | bytes 196616 | tf_op jit(solution)/shard_map/ppermute | solution.py:39
  40.9 0.1 slice.47
  40.9 0.3 copy.47
  41.2 1.6 %collective-permute-done.5 = bf16[256,128]{1,0:T(8,128)(2,1)S(1)} collective-permute-done((bf16[256,128]{1,0:T(8,128)(2,1)S(1)}, bf16[256,128]{1,0:T(8,128)(2,1)S(1)}, u32[]{:S(2)}, u32[]{:S(2)}) %collective-permute-start.5) | collective-permute-done | bytes 65568 | tf_op jit(solution)/shard_map/ppermute | solution.py:37
  42.8 0.0 collective-permute-done.6
  42.8 0.1 copy.48
  42.9 0.1 copy.49
  43.0 1.6 %scatter_fusion = f32[256,768]{0,1:T(8,128)S(1)} fusion(f32[256,768]{0,1:T(8,128)S(1)} %copy.47, s32[128]{0:T(128)S(1)} %get-tuple-element.19, f32[128,256]{1,0:T(8,128)S(1)} %copy.48), kind=kCustom, calls=%fused_computation.3 | custom fusion | flops 32768 | bytes 393728 | tf_op jit(solution)/shard_map/scatter-add | solution.py:120
  44.6 1.6 %scatter_fusion.1 = f32[256,768]{0,1:T(8,128)S(1)} fusion(f32[256,768]{0,1:T(8,128)S(1)} %scatter_fusion, s32[128]{0:T(128)S(1)} %get-tuple-element.18, f32[128,256]{1,0:T(8,128)S(1)} %copy.49), kind=kCustom, calls=%fused_computation.4 | custom fusion | flops 32768 | bytes 393728 | tf_op jit(solution)/shard_map/scatter-add | solution.py:121
  46.2 1.1 %copy.50 = f32[256,768]{1,0:T(8,128)} copy(f32[256,768]{0,1:T(8,128)S(1)} %scatter_fusion.1) | data formatting | bytes 1572864 | tf_op jit(solution)/shard_map/scatter-add | solution.py:121
  (22 shorter events, 0.3 us)
Async XLA Ops:
  0.0 12.4 %copy-start = (bf16[1024,384]{1,0:T(8,128)(2,1)S(1)}, bf16[1024,384]{1,0:T(8,128)(2,1)}, u32[]{:S(2)}) copy-start(bf16[1024,384]{1,0:T(8,128)(2,1)} %param.9) | copy-start | bytes 2359300
  0.0 10.5 %copy-start.1 = (s32[384,1]{0,1:T(1,128)S(1)}, s32[384,1]{0,1:T(1,128)}, u32[]{:S(2)}) copy-start(s32[384,1]{0,1:T(1,128)} %param.12) | copy-start | bytes 4612
  0.0 12.3 %copy-start.3 = (s32[2,3]{1,0:T(2,128)S(1)}, s32[2,3]{1,0:T(2,128)}, u32[]{:S(2)}) copy-start(s32[2,3]{1,0:T(2,128)} %param.11) | copy-start | bytes 76
  3.0 9.3 %collective-permute-start = (bf16[256,128]{0,1:T(8,128)(2,1)S(1)}, bf16[256,128]{0,1:T(8,128)(2,1)S(1)}, u32[]{:S(2)}, u32[]{:S(2)}) collective-permute-start(bf16[256,128]{0,1:T(8,128)(2,1)S(1)} %select_bitcast_fusion.1), channel_id=1, source_target_pairs={{0,1},{1,2},{2,3},{3,4},{4,5},{5,6},{6,7},{7,8},{8,9},{9,10},{10,1... | collective-permute-start | bytes 196616 | tf_op jit(solution)/shard_map/ppermute | solution.py:37
  4.5 7.9 %collective-permute-start.1 = (bf16[256,128]{0,1:T(8,128)(2,1)S(1)}, bf16[256,128]{0,1:T(8,128)(2,1)S(1)}, u32[]{:S(2)}, u32[]{:S(2)}) collective-permute-start(bf16[256,128]{0,1:T(8,128)(2,1)S(1)} %select_bitcast_fusion), channel_id=1, source_target_pairs={{1,0},{2,1},{3,2},{4,3},{5,4},{6,5},{7,6},{8,7},{9,8},{10,9},{11,1... | collective-permute-start | bytes 196616 | tf_op jit(solution)/shard_map/ppermute | solution.py:39
  13.8 5.0 %collective-permute-start.3 = (bf16[256,128]{1,0:T(8,128)(2,1)S(1)}, bf16[256,128]{1,0:T(8,128)(2,1)S(1)}, u32[]{:S(2)}, u32[]{:S(2)}) collective-permute-start(bf16[256,128]{1,0:T(8,128)(2,1)S(1)} %bitcast.111), channel_id=1, source_target_pairs={{0,2},{1,3},{2,0},{3,1},{4,6},{5,7},{6,4},{7,5},{8,10},{9,11},{10,... | collective-permute-start | bytes 196616 | tf_op jit(solution)/shard_map/ppermute | solution.py:25
  13.9 4.9 %collective-permute-start.4 = (bf16[256,128]{1,0:T(8,128)(2,1)S(1)}, bf16[256,128]{1,0:T(8,128)(2,1)S(1)}, u32[]{:S(2)}, u32[]{:S(2)}) collective-permute-start(bf16[256,128]{1,0:T(8,128)(2,1)S(1)} %bitcast.112), channel_id=1, source_target_pairs={{0,3},{1,0},{2,1},{3,2},{4,7},{5,4},{6,5},{7,6},{8,11},{9,8},{10,9... | collective-permute-start | bytes 196616 | tf_op jit(solution)/shard_map/ppermute | solution.py:25
  14.5 4.4 %collective-permute-start.2 = (bf16[256,128]{1,0:T(8,128)(2,1)S(1)}, bf16[256,128]{1,0:T(8,128)(2,1)S(1)}, u32[]{:S(2)}, u32[]{:S(2)}) collective-permute-start(bf16[256,128]{1,0:T(8,128)(2,1)S(1)} %bitcast.113), channel_id=1, source_target_pairs={{0,1},{1,2},{2,3},{3,0},{4,5},{5,6},{6,7},{7,4},{8,9},{9,10},{10,1... | collective-permute-start | bytes 196616 | tf_op jit(solution)/shard_map/ppermute | solution.py:25
  34.6 6.2 %copy-start.2 = (s32[2,128]{1,0:T(2,128)S(1)}, s32[2,128]{1,0:T(2,128)}, u32[]{:S(2)}) copy-start(s32[2,128]{1,0:T(2,128)} %param.13) | copy-start | bytes 3076
  35.5 7.3 %collective-permute-start.5 = (bf16[256,128]{1,0:T(8,128)(2,1)S(1)}, bf16[256,128]{1,0:T(8,128)(2,1)S(1)}, u32[]{:S(2)}, u32[]{:S(2)}) collective-permute-start(bf16[256,128]{1,0:T(8,128)(2,1)S(1)} %get-tuple-element.10), channel_id=1, source_target_pairs={{0,1},{1,2},{2,3},{3,4},{4,5},{5,6},{6,7},{7,8},{8,9},{9,10},{10,1... | collective-permute-start | bytes 196616 | tf_op jit(solution)/shard_map/ppermute | solution.py:37
  35.5 7.3 %collective-permute-start.6 = (bf16[256,128]{1,0:T(8,128)(2,1)S(1)}, bf16[256,128]{1,0:T(8,128)(2,1)S(1)}, u32[]{:S(2)}, u32[]{:S(2)}) collective-permute-start(bf16[256,128]{1,0:T(8,128)(2,1)S(1)} %get-tuple-element.11), channel_id=1, source_target_pairs={{1,0},{2,1},{3,2},{4,3},{5,4},{6,5},{7,6},{8,7},{9,8},{10,9},{11,1... | collective-permute-start | bytes 196616 | tf_op jit(solution)/shard_map/ppermute | solution.py:39
